TPU v7x, 16 devices: a whole 2x2x2 slice. The times are simulated.
16 devices in a mesh: etp: 4 (over z, y), ep: 4 (over x, core).
Axes of the slice: x: 2, y: 2, z: 2, core: 2. Of those that a mesh axis runs over, the one named last changes fastest.
Arguments:
- hidden: bfloat16 [65536, 256], P(('ep', 'etp'))
- w_router: float32 [256, 64], replicated
- expert_ids: int32 [65536, 2], P(('ep', 'etp'))
- d_out: bfloat16 [65536, 256], P(('ep', 'etp'))
- w_gate: bfloat16 [64, 256, 1024], P('ep', None, 'etp')
- w_up: bfloat16 [64, 256, 1024], P('ep', None, 'etp')
- w_down: bfloat16 [64, 1024, 256], P('ep', 'etp')
Outputs:
- output 1: bfloat16 [65536, 256], P(('ep', 'etp'))
- output 2: bfloat16 [65536, 256], P(('ep', 'etp'))
- output 3: float32 [256, 64], replicated
- output 4: float32 [], replicated
- output 5: float32 [64, 256, 1024], P('ep', None, 'etp')
- output 6: float32 [64, 256, 1024], P('ep', None, 'etp')
- output 7: float32 [64, 1024, 256], P('ep', 'etp')
All inputs are finite; a program needn't handle non-finite values.
Results may differ from a plain program's by a relative error of at most 0.00894483.
Values are sent between devices in bfloat16 or wider.
A program may use at most 1 GiB of HBM per device.

v0:
```python
import functools
import jax
import jax.numpy as jnp
from jax import lax
from jax.sharding import PartitionSpec as P

AUX_COEF = 0.01
OUT_SCALE = 2.0


def route_terms(logits, expert_ids):
    prob_vals = jax.nn.softmax(logits, axis=-1)
    picked = jnp.take_along_axis(prob_vals, expert_ids, axis=1)
    return picked / jnp.sum(picked, axis=1, keepdims=True), jnp.sum(prob_vals, axis=0)


def solution(mesh):
    ep_size = mesh.shape["ep"]
    etp_size = mesh.shape["etp"]
    n_dev = ep_size * etp_size
    all_axes = ("ep", "etp")
    tok_spec = P(all_axes, None)
    gate_spec = P("ep", None, "etp")
    down_spec = P("ep", "etp", None)

    def layer(hidden, w_router, expert_ids, d_out, w_gate, w_up, w_down):
        tok_rows, d_model = hidden.shape
        n_experts = w_router.shape[1]
        n_tokens = tok_rows * n_dev
        n_assign = 2 * tok_rows
        capacity = (5 * n_tokens + 2 * n_experts - 1) // (2 * n_experts)
        per_expert = 7 * tok_rows // (2 * n_experts)
        block_idx = lax.axis_index("ep") * etp_size + lax.axis_index("etp")

        hidden_f = hidden.astype(jnp.float32)
        logits = jnp.dot(hidden_f, w_router, preferred_element_type=jnp.float32)
        (gate_vals, prob_sum), route_vjp = jax.vjp(functools.partial(route_terms, expert_ids=expert_ids), logits)

        flat_ids = expert_ids.reshape(-1)
        one_hot = (flat_ids[:, None] == jnp.arange(n_experts, dtype=jnp.int32)[None, :]).astype(jnp.int32)
        local_pos = jnp.sum((jnp.cumsum(one_hot, axis=0) - one_hot) * one_hot, axis=1)
        count_table = lax.all_gather(jnp.sum(one_hot, axis=0), all_axes)
        earlier = (jnp.arange(n_dev) < block_idx)[:, None]
        prefix = jnp.sum(jnp.where(earlier, count_table, 0), axis=0)
        total_count = jnp.sum(count_table, axis=0)
        kept_mask = prefix[flat_ids] + local_pos < capacity
        dest_rows = jnp.where(kept_mask, flat_ids * per_expert + local_pos, n_experts * per_expert)
        source = jnp.full((n_experts * per_expert,), n_assign, jnp.int32).at[dest_rows].set(jnp.arange(n_assign, dtype=jnp.int32), mode="drop")

        def dispatch(values, row_index):
            send_buf = jnp.take(values, row_index, axis=0, mode="fill", fill_value=0).reshape(n_experts, per_expert, d_model)
            received = lax.all_to_all(send_buf, "ep", 0, 1, tiled=True)
            return lax.all_gather(received, "etp", axis=1, tiled=True)

        def combine(part_out):
            summed = lax.psum_scatter(part_out, "etp", scatter_dimension=1, tiled=True).astype(jnp.bfloat16)
            returned = lax.all_to_all(summed, "ep", 1, 0, tiled=True).reshape(n_experts * per_expert, d_model)
            return jnp.take(returned, dest_rows, axis=0, mode="fill", fill_value=0).reshape(tok_rows, 2, d_model)

        x_in = dispatch(hidden, source // 2)
        act_a = jnp.einsum("erd,edf->erf", x_in, w_gate, preferred_element_type=jnp.float32)
        act_b = jnp.einsum("erd,edf->erf", x_in, w_up, preferred_element_type=jnp.float32)
        sig_a = jax.nn.sigmoid(act_a)
        silu_a = act_a * sig_a
        inner_act = (silu_a * act_b).astype(jnp.bfloat16)
        y_pair = combine(jnp.einsum("erf,efd->erd", inner_act, w_down, preferred_element_type=jnp.float32))

        d_mix = OUT_SCALE * d_out.astype(jnp.float32)
        output = (hidden_f + OUT_SCALE * jnp.sum(gate_vals[:, :, None] * y_pair, axis=1)).astype(jnp.bfloat16)
        d_gates = jnp.sum(d_mix[:, None, :] * y_pair, axis=2)
        dy_assign = (gate_vals[:, :, None] * d_mix[:, None, :]).astype(jnp.bfloat16).reshape(n_assign, d_model)
        dy_in = dispatch(dy_assign, source)
        d_inner = jnp.einsum("erd,efd->erf", dy_in, w_down, preferred_element_type=jnp.float32)
        d_act_a = (d_inner * act_b * sig_a * (1.0 + act_a * (1.0 - sig_a))).astype(jnp.bfloat16)
        d_act_b = (d_inner * silu_a).astype(jnp.bfloat16)
        dx_part = jnp.einsum("erf,edf->erd", d_act_a, w_gate, preferred_element_type=jnp.float32) + jnp.einsum("erf,edf->erd", d_act_b, w_up, preferred_element_type=jnp.float32)
        dx_pair = combine(dx_part)
        g_gate = jnp.einsum("erd,erf->edf", x_in, d_act_a, preferred_element_type=jnp.float32)
        g_up = jnp.einsum("erd,erf->edf", x_in, d_act_b, preferred_element_type=jnp.float32)
        g_down = jnp.einsum("erf,erd->efd", inner_act, dy_in, preferred_element_type=jnp.float32)

        route_frac = total_count.astype(jnp.float32) / (2 * n_tokens)
        mean_prob = lax.psum(prob_sum, all_axes) / n_tokens
        aux_loss = AUX_COEF * n_experts * jnp.sum(route_frac * mean_prob)
        (d_logits,) = route_vjp((d_gates, (AUX_COEF * n_experts / n_tokens) * route_frac))
        d_router = lax.psum(jnp.einsum("td,te->de", hidden_f, d_logits, preferred_element_type=jnp.float32), all_axes)
        d_hidden = (d_out.astype(jnp.float32) + jnp.sum(dx_pair, axis=1, dtype=jnp.float32) + jnp.einsum("te,de->td", d_logits, w_router, preferred_element_type=jnp.float32)).astype(jnp.bfloat16)
        return output, d_hidden, d_router, aux_loss, g_gate, g_up, g_down

    return jax.shard_map(layer, mesh=mesh, in_specs=(tok_spec, P(), tok_spec, tok_spec, gate_spec, gate_spec, down_spec), out_specs=(tok_spec, tok_spec, P(), P(), gate_spec, gate_spec, down_spec), check_vma=False)
```

profile of v0, /device:TPU:0, one launch (start us, length us, event | category | flops | bytes accessed | tf_op | source)
XLA Modules:
  0.0 2259.1 jit_solution(12763748909723815108)
XLA Ops:
  7.2 2.9 copy.97
  10.1 2.7 eq.29
  12.8 2.7 eq.25
  15.6 3.1 reshape.199
  20.2 36.7 %reduce-window.6 = s32[64,64,128]{2,1,0:T(8,128)} reduce-window(s32[64,64,128]{2,1,0:T(8,128)} %fusion.4, s32[]{:T(128)} %constant.55.clone.1), window={size=1x1x128 pad=0_0x0_0x127_0}, to_apply=%region_5.6 | reduce-window | flops 66584576 | bytes 4194308 | tf_op jit(solution)/shard_map/reduce-window
  56.9 3.3 slice_reduce_fusion
  62.3 2.4 convert_reduce_fusion
  66.2 34.9 %all-reduce = s32[1024]{0:T(1024)S(1)} all-reduce(s32[1024]{0:T(1024)S(1)} %dynamic-update-slice), channel_id=2, replica_groups=mesh['etp'=4,'ep'=4] {'ep','etp'}, use_global_device_ids=true, to_apply=%add | all-reduce | flops 1024 | bytes 8192
  104.6 4.6 compare_select_fusion.3
  109.2 5.8 compare_reduce_fusion.56
  115.1 36.4 %compare_and_fusion.2 = (pred[8192]{0:T(1024)(128)(4,1)}, s32[8192]{0:T(1024)S(1)}) fusion(s32[8192]{0:T(1024)S(1)} %get-tuple-element.9, s32[8192]{0:T(1024)S(1)} %eq.25, pred[8192]{0:T(1024)(128)(4,1)S(1)} %get-tuple-element.66, pred[8192]{0:T(1024)(128)(4,1)S(1)} %get-tuple-element.65, pred[8192]{0:T(1024)(128)(4,1)S(1)} %get-tuple-element.64, ...), kind=kLoop, calls=%fused_computation.132 | loop fusion | flops 557056 | bytes 606436 | tf_op jit(solution)/shard_map/jit(_take)/and | solution.py:58
  152.1 30.5 %scatter_custom_fusion = s32[14336]{0:T(1024)S(1)} fusion(s32[8192]{0:T(1024)S(1)} %bitcast.152, s32[8192]{0:T(1024)S(1)} %iota.17, s32[]{:T(128)} %constant.67.clone.1), kind=kCustom, calls=%fused_computation.134 | custom fusion | bytes 57348 | tf_op jit(solution)/shard_map/scatter | solution.py:48
  184.0 55.2 %gather_fusion = bf16[14336,256]{1,0:T(8,128)(2,1)} fusion(bf16[4096,256]{1,0:T(8,128)(2,1)} %param.9, s32[14336]{0:T(1024)S(1)} %get-tuple-element.83), kind=kCustom, calls=%fused_computation.2 | custom fusion | bytes 14737408 | tf_op jit(solution)/shard_map/jit(_take)/gather | solution.py:51
  239.3 6.5 broadcast_select_fusion.1
  245.8 85.2 %all_to_all.66 = bf16[64,224,256]{2,1,0:T(8,128)(2,1)S(1)} all-to-all(bf16[64,224,256]{2,1,0:T(8,128)(2,1)S(1)} %broadcast_select_fusion.1), channel_id=1, replica_groups=mesh['etp'=4,'ep'=4] {'ep'}, dimensions={0} | all-to-all | bytes 14680064 | tf_op jit(solution)/shard_map/all_to_all | solution.py:52
  330.9 3.6 copy.100
  337.3 2.7 reshape.312
  340.0 2.3 fusion.22
  343.4 65.5 %gather_fusion.2 = f32[8192]{0:T(1024)S(1)} fusion(f32[4096,64]{0,1:T(8,128)S(1)} %get-tuple-element.70, s32[8192]{0:T(1024)S(1)} %reshape.312), kind=kCustom, calls=%fused_computation.4 | custom fusion | bytes 131072 | tf_op jit(solution)/shard_map/jvp(jit(take_along_axis))/gather | solution.py:13
  409.0 3.4 reshape.315
  412.4 2.2 copy.95
  417.3 2.7 mul.144
  421.9 4.5 mul.147
  426.4 10.9 mul.148
  437.4 5.4 multiply_convert_fusion.3
  442.8 56.1 %gather_fusion.1 = bf16[14336,256]{1,0:T(8,128)(2,1)} fusion(bf16[8192,256]{1,0:T(8,128)(2,1)} %multiply_convert_fusion.3, s32[14336]{0:T(1024)S(1)} %copy-done.30), kind=kCustom, calls=%fused_computation.3 | custom fusion | bytes 14737408 | tf_op jit(solution)/shard_map/jit(_take)/gather | solution.py:51
  498.9 6.5 broadcast_select_fusion
  505.4 84.5 %all_to_all.67 = bf16[64,224,256]{2,1,0:T(8,128)(2,1)S(1)} all-to-all(bf16[64,224,256]{2,1,0:T(8,128)(2,1)S(1)} %broadcast_select_fusion), channel_id=1, replica_groups=mesh['etp'=4,'ep'=4] {'ep'}, dimensions={0} | all-to-all | bytes 14680064 | tf_op jit(solution)/shard_map/all_to_all | solution.py:52
  590.0 3.7 copy.104
  593.9 29.9 %fusion.23 = f32[16,3584,256]{2,1,0:T(8,128)} fusion(bf16[16,3584,256]{2,1,0:T(8,128)(2,1)} %all-gather.4.cloned.1.call-done, bf16[16,256,256]{2,1,0:T(8,128)(2,1)} %param.13), kind=kOutput, calls=%fused_computation.154 | convolution fusion | flops 7516192768 | bytes 90177536 | tf_op jit(solution)/shard_map/erd,edf->erf/dot_general | solution.py:61
  623.9 29.2 %fusion.24 = f32[16,3584,256]{2,1,0:T(8,128)} fusion(bf16[16,3584,256]{2,1,0:T(8,128)(2,1)} %all-gather.4.cloned.1.call-done, bf16[16,256,256]{2,1,0:T(8,128)(2,1)S(1)} %copy-done.5), kind=kOutput, calls=%fused_computation.155 | convolution fusion | flops 7516192768 | bytes 90177536 | tf_op jit(solution)/shard_map/erd,edf->erf/dot_general | solution.py:62
  653.0 199.6 %all-gather.6.cloned.1.call-done = bf16[16,3584,256]{2,1,0:T(8,128)(2,1)} async-done(((bf16[16,896,256]{2,1,0:T(8,128)(2,1)}), bf16[16,3584,256]{2,1,0:T(8,128)(2,1)}) %all-gather.6.cloned.1.call-update) | async-done | bytes 29360144 | tf_op jit(solution)/shard_map/all_gather | solution.py:53
  852.6 76.0 %multiply_convert_fusion = (bf16[16,3584,256]{2,1,0:T(8,128)(2,1)}, bf16[16,3584,256]{2,1,0:T(8,128)(2,1)}, bf16[16,3584,256]{2,1,0:T(8,128)(2,1)}) fusion(f32[16,3584,256]{2,1,0:T(8,128)} %fusion.23, f32[16,3584,256]{2,1,0:T(8,128)} %fusion.24, bf16[16,3584,256]{2,1,0:T(8,128)(2,1)} %all-gather.6.cloned.1.call-done, bf16[16,256,256]{2,1,0:T(8,128)(2,1)S(1)} %copy-done), kind=kOutput, calls=%fused_computation.7 | convolution fusion | flops 7736393728 | bytes 236978176 | tf_op jit(solution)/shard_map/erd,efd->erf/dot_general | solution.py:73
  928.6 29.2 %fusion.25 = f32[16,3584,256]{2,1,0:T(8,128)} fusion(bf16[16,3584,256]{2,1,0:T(8,128)(2,1)} %get-tuple-element.79, bf16[16,256,256]{2,1,0:T(8,128)(2,1)S(1)} %copy-done), kind=kOutput, calls=%fused_computation.156 | convolution fusion | flops 7516192768 | bytes 90177536 | tf_op jit(solution)/shard_map/erf,efd->erd/dot_general | solution.py:66
  958.1 30.0 %fusion.26 = f32[16,3584,256]{2,1,0:T(8,128)} fusion(bf16[16,3584,256]{2,1,0:T(8,128)(2,1)} %get-tuple-element.78, bf16[16,256,256]{2,1,0:T(8,128)(2,1)} %param.13), kind=kOutput, calls=%fused_computation.157 | convolution fusion | flops 7516192768 | bytes 90177536 | tf_op jit(solution)/shard_map/erf,edf->erd/dot_general | solution.py:76
  988.0 48.9 %convolution_add_fusion = f32[16,3584,256]{2,1,0:T(8,128)} fusion(f32[16,3584,256]{2,1,0:T(8,128)} %fusion.26, bf16[16,3584,256]{2,1,0:T(8,128)(2,1)} %get-tuple-element.77, bf16[16,256,256]{2,1,0:T(8,128)(2,1)S(1)} %copy-done.6), kind=kOutput, calls=%fused_computation.12 | convolution fusion | flops 7530872832 | bytes 148897792 | tf_op jit(solution)/shard_map/erf,edf->erd/dot_general | solution.py:76
  1037.6 32.5 %psum.15 = f32[64]{0:T(128)S(1)} all-reduce(f32[64]{0:T(128)S(1)} %copy-done.38), channel_id=1, replica_groups=mesh['etp'=4,'ep'=4] {'ep','etp'}, use_global_device_ids=true, to_apply=%region_20.22 | all-reduce | flops 64 | bytes 512 | tf_op jit(solution)/shard_map/psum | solution.py:83
  1070.7 376.5 %reduce-scatter.3.cloned.1.call-done = f32[16,896,256]{2,1,0:T(8,128)} async-done(((f32[16,3584,256]{2,1,0:T(8,128)}), f32[16,896,256]{2,1,0:T(8,128)}) %reduce-scatter.3.cloned.1.call-update) | async-done | bytes 14680080 | tf_op jit(solution)/shard_map/reduce_scatter | solution.py:56
  1447.2 9.0 convert_element_type.62
  1456.3 10.2 copy.101
  1466.4 6.0 all-to-all-start.1
  1475.3 2.7 reshape.326
  1479.4 22.5 fusion.29
  1501.9 436.0 %reduce-scatter.5.cloned.1.call-done = f32[16,896,256]{2,1,0:T(8,128)} async-done(((f32[16,3584,256]{2,1,0:T(8,128)}), f32[16,896,256]{2,1,0:T(8,128)}) %reduce-scatter.5.cloned.1.call-update) | async-done | bytes 14680080 | tf_op jit(solution)/shard_map/reduce_scatter | solution.py:56
  1937.9 9.2 convert_element_type.70
  1947.1 10.3 copy.105
  1957.3 5.5 all-to-all-start.3
  1963.0 22.5 fusion.27
  1985.5 22.5 fusion.28
  2008.0 9.1 copy.102
  2017.0 35.0 %gather_fusion.3 = bf16[8192,256]{1,0:T(8,128)(2,1)} fusion(bf16[14336,256]{1,0:T(8,128)(2,1)} %bitcast.140, s32[8192]{0:T(1024)S(1)} %broadcast_clamp_fusion.1), kind=kCustom, calls=%fused_computation.clone | custom fusion | bytes 8421376 | tf_op jit(solution)/shard_map/jit(_take)/gather | solution.py:58
  2052.0 6.5 multiply_reduce_fusion
  2058.6 3.4 reduce_sum.139
  2066.3 2.7 reshape.328
  2069.0 44.6 %scatter_fusion = f32[262144]{0:T(1024)S(1)} fusion(f32[262144]{0:T(1024)S(1)} %bitcast.138, s32[8192]{0:T(1024)S(1)} %reshape.326, f32[8192]{0:T(1024)S(1)} %reshape.328), kind=kCustom, calls=%fused_computation.6 | custom fusion | flops 8192 | bytes 131072
  2114.4 2.7 convolution_bitcast_fusion
  2117.2 9.0 copy.106
  2126.1 35.2 %gather_fusion.4 = bf16[8192,256]{1,0:T(8,128)(2,1)} fusion(bf16[14336,256]{1,0:T(8,128)(2,1)} %bitcast.139, s32[8192]{0:T(1024)S(1)} %copy-done.22), kind=kCustom, calls=%fused_computation.1.clone | custom fusion | bytes 8421376 | tf_op jit(solution)/shard_map/jit(_take)/gather | solution.py:58
  2161.3 10.8 select_convert_fusion
  2172.1 10.6 reshape.208
  2182.7 10.6 reshape.207
  2193.2 23.8 %multiply_reduce_fusion.1 = f32[4096,256]{1,0:T(8,128)S(1)} fusion(f32[4096,2,256]{2,1,0:T(2,128)} %reshape.207, f32[4096,2]{1,0:T(8,128)} %copy.96), kind=kLoop, calls=%fused_computation.15 | loop fusion | flops 3145728 | bytes 12615680 | tf_op jit(solution)/shard_map/reduce_sum | solution.py:69
  2219.1 25.0 %reduce_sum.136 = f32[4096,256]{1,0:T(8,128)} reduce(f32[4096,2,256]{2,1,0:T(2,128)} %reshape.208, f32[]{:T(128)} %constant.65.clone.1), dimensions={1}, to_apply=%region_12.14 | reduce | flops 1048576 | bytes 12582916 | tf_op jit(solution)/shard_map/reduce_sum | solution.py:87
  2244.1 5.4 fusion.1
  (145 shorter events, 32.5 us)
Async XLA Ops:
  7.2 845.5 %copy-start = (bf16[16,256,256]{2,1,0:T(8,128)(2,1)S(1)}, bf16[16,256,256]{2,1,0:T(8,128)(2,1)}, u32[]{:S(2)}) copy-start(bf16[16,256,256]{2,1,0:T(8,128)(2,1)} %param.15) | copy-start | bytes 6291460
  7.2 586.7 %all-gather.4.cloned.1.call-start = ((), (), s32[]{:S(2)}) async-start(), calls=%async_computation.6 | async-start | bytes 36700160 | tf_op jit(solution)/shard_map/all_gather | solution.py:53
  15.6 99.5 %copy-start.8 = (s32[8192]{0:T(1024)}, s32[8192]{0:T(1024)S(1)}, u32[]{:S(2)}) copy-start(s32[8192]{0:T(1024)S(1)} %eq.25) | copy-start | bytes 98308
  56.9 7.9 copy-start.39
  64.7 174.5 %copy-start.13 = (s32[8192]{0:T(1024)}, s32[8192]{0:T(1024)S(1)}, u32[]{:S(2)}) copy-start(s32[8192]{0:T(1024)S(1)} %get-tuple-element.9) | copy-start | bytes 98308
  151.5 0.6 copy-start.19
  334.5 0.8 copy-start.10
  334.5 5.5 copy-start.25
  334.5 518.1 %all-gather.6.cloned.1.call-start = ((), (), s32[]{:S(2)}) async-start(), calls=%async_computation.8 | async-start | bytes 36700160 | tf_op jit(solution)/shard_map/all_gather | solution.py:53
  342.4 1.0 copy-start.3
  342.4 1.0 copy-start.15
  342.6 0.8 copy-start.27
  409.0 5.6 copy-start.11
  414.7 0.6 copy-start.17
  414.7 0.6 copy-start.23
  426.4 10.9 copy-start.34
  437.4 5.4 copy-start.30
  593.7 853.6 %reduce-scatter.3.cloned.1.call-start = ((), (), s32[]{:S(2)}) async-start(), calls=%async_computation.7 | async-start | bytes 73400320 | tf_op jit(solution)/shard_map/reduce_scatter | solution.py:56
  593.9 30.0 %copy-start.5 = (bf16[16,256,256]{2,1,0:T(8,128)(2,1)S(1)}, bf16[16,256,256]{2,1,0:T(8,128)(2,1)}, u32[]{:S(2)}) copy-start(bf16[16,256,256]{2,1,0:T(8,128)(2,1)} %param.14) | copy-start | bytes 6291460
  957.8 980.1 %reduce-scatter.5.cloned.1.call-start = ((), (), s32[]{:S(2)}) async-start(), calls=%async_computation.9 | async-start | bytes 73400320 | tf_op jit(solution)/shard_map/reduce_scatter | solution.py:56
  958.1 30.0 %copy-start.6 = (bf16[16,256,256]{2,1,0:T(8,128)(2,1)S(1)}, bf16[16,256,256]{2,1,0:T(8,128)(2,1)}, u32[]{:S(2)}) copy-start(bf16[16,256,256]{2,1,0:T(8,128)(2,1)} %param.14) | copy-start | bytes 6291460
  1037.0 0.6 copy-start.38
  1037.0 33.1 %copy-start.35 = (s32[64]{0:T(128)S(1)}, s32[64]{0:T(128)}, u32[]{:S(2)}) copy-start(s32[64]{0:T(128)} %get-tuple-element.67) | copy-start | bytes 772
  1466.4 6.4 copy-start.12
  1466.4 6.5 copy-start.37
  1466.4 6.7 copy-start.36
  1466.4 490.9 %all-to-all-start.1 = ((bf16[16,896,256]{2,0,1:T(8,128)(2,1)}), bf16[16,896,256]{2,0,1:T(8,128)(2,1)}, u32[]{:S(2)}, u32[]{:S(2)}) async-start(bf16[16,896,256]{2,0,1:T(8,128)(2,1)} %copy.101), calls=%async_computation.2 | async-start | bytes 14680064 | tf_op jit(solution)/shard_map/all_to_all | solution.py:57
  1472.4 6.3 copy-start.24
  1472.4 6.3 copy-start.28
  1472.4 6.9 copy-start.9
  1472.4 6.9 copy-start.14
  1472.4 6.9 copy-start.20
  1479.4 537.6 %copy-start.21 = (s32[8192]{0:T(1024)}, s32[8192]{0:T(1024)S(1)}, u32[]{:S(2)}) copy-start(s32[8192]{0:T(1024)S(1)} %broadcast_clamp_fusion.1) | copy-start | bytes 98308
  1957.3 159.8 %all-to-all-start.3 = ((bf16[16,896,256]{2,0,1:T(8,128)(2,1)}), bf16[16,896,256]{2,0,1:T(8,128)(2,1)}, u32[]{:S(2)}, u32[]{:S(2)}) async-start(bf16[16,896,256]{2,0,1:T(8,128)(2,1)} %copy.105), calls=%async_computation.5 | async-start | bytes 14680064 | tf_op jit(solution)/shard_map/all_to_all | solution.py:57
  1962.8 286.7 %all-reduce.3.cloned.1.call-start = ((), (), s32[]{:S(2)}) async-start(), calls=%async_computation.10 | async-start | bytes 131072 | tf_op jit(solution)/shard_map/psum | solution.py:86
  2017.0 35.0 %copy-start.31 = (pred[8192]{0:T(1024)(128)(4,1)S(1)}, pred[8192]{0:T(1024)(128)(4,1)}, u32[]{:S(2)}) copy-start(pred[8192]{0:T(1024)(128)(4,1)} %get-tuple-element.73) | copy-start | bytes 24580
  2058.6 5.6 copy-start.18
  2069.0 44.9 %copy-start.4 = (f32[4096,64]{0,1:T(8,128)S(1)}, f32[4096,64]{0,1:T(8,128)}, u32[]{:S(2)}) copy-start(f32[4096,64]{0,1:T(8,128)} %copy-done.3) | copy-start | bytes 3145732
  2069.0 44.9 %copy-start.16 = (f32[4096]{0:T(1024)S(1)}, f32[4096]{0:T(1024)}, u32[]{:S(2)}) copy-start(f32[4096]{0:T(1024)} %copy-done.15) | copy-start | bytes 49156
  2069.0 44.9 %copy-start.33 = (f32[4096]{0:T(1024)S(1)}, f32[4096]{0:T(1024)}, u32[]{:S(2)}) copy-start(f32[4096]{0:T(1024)} %multiply_divide_fusion) | copy-start | bytes 49156
  2113.7 0.7 copy-start.29
  2113.9 12.2 copy-start.7
  2117.1 9.0 copy-start.22
  2126.1 35.2 %copy-start.32 = (pred[8192]{0:T(1024)(128)(4,1)S(1)}, pred[8192]{0:T(1024)(128)(4,1)}, u32[]{:S(2)}) copy-start(pred[8192]{0:T(1024)(128)(4,1)} %get-tuple-element.73) | copy-start | bytes 24580
  2193.2 23.8 %copy-start.2 = (bf16[4096,256]{1,0:T(8,128)(2,1)S(1)}, bf16[4096,256]{1,0:T(8,128)(2,1)}, u32[]{:S(2)}) copy-start(bf16[4096,256]{1,0:T(8,128)(2,1)} %param.9) | copy-start | bytes 6291460
  2219.1 25.0 %copy-start.26 = (f32[256,64]{0,1:T(8,128)S(1)}, f32[256,64]{0,1:T(8,128)}, u32[]{:S(2)}) copy-start(f32[256,64]{0,1:T(8,128)} %param.10) | copy-start | bytes 196612
  2219.1 31.9 %copy-start.1 = (bf16[16,256,256]{2,1,0:T(8,128)(2,1)S(1)}, bf16[16,256,256]{2,1,0:T(8,128)(2,1)}, u32[]{:S(2)}) copy-start(bf16[16,256,256]{2,1,0:T(8,128)(2,1)} %param.15) | copy-start | bytes 6291460
Sparse Core Ops, SparseCore 0:
  334.7 257.6 all-gather.3
  594.2 258.3 all-gather.5
  957.9 489.2 reduce-scatter.2
  1450.2 487.6 reduce-scatter.4
  2117.3 65.3 all-reduce.2
where the time goes:
time: 2270 us; the launch traced here: 2260 us
  waiting for transfers between devices  1010 us (44%)
  local copies, waits for them, and re-layouts  413 us (18%)
  matrix products  321 us (14%)
  other arithmetic  246 us (11%)
  blocking collectives  237 us (10%)
    reduce_scatter x2, waiting for transfers between devices, combine(): lax.psum_scatter(part_out, 'etp', scatter_dimension=1, tiled=True)  813 us
    all_gather x2, waiting for transfers between devices, dispatch(): return lax.all_gather(received, 'etp', axis=1, tiled=True)  200 us
    all_to_all x2, blocking collectives, dispatch(): received = lax.all_to_all(send_buf, 'ep', 0, 1, tiled=True)  170 us
    gather x2, local copies, waits for them, and re-layouts, dispatch(): jnp.take(values, row_index, axis=0, mode='fill', fill_value=0)  111 us
    dot_general x1, matrix products, layer(): jnp.einsum('erd,efd->erf', dy_in, w_down, preferred_element_type=jnp.floa...  76 us
    gather x7, local copies, waits for them, and re-layouts, route_terms(): picked = jnp.take_along_axis(prob_vals, expert_ids, axis=1)  75.9 us
    gather x2, local copies, waits for them, and re-layouts, combine(): jnp.take(returned, dest_rows, axis=0, mode='fill', fill_value=0)  70.2 us
    dot_general x1, matrix products, layer(): jnp.einsum('erf,edf->erd', d_act_b, w_up, preferred_element_type=jnp.floa...  48.9 us
  transfers between devices with their start and end apart: 7, of which 3 were waited for; matrix products, arithmetic and copies ran while one was open for 29% of the time, Pallas kernels for 0%

commit v1 on v0

v1 whole, which is shorter than its diff:
```python
import functools
import jax
import jax.numpy as jnp
from jax import lax
from jax.experimental import pallas as pl
from jax.experimental.pallas import tpu as pltpu
from jax.sharding import PartitionSpec as P

AUX_COEF = 0.01
OUT_SCALE = 2.0
F32 = jnp.float32
BF16 = jnp.bfloat16
HI = lax.Precision.HIGHEST
MESH = pl.DeviceIdType.MESH
NT = (((1,), (1,)), ((), ()))
TN = (((0,), (0,)), ((), ()))


def dot(a, b, dims=(((1,), (0,)), ((), ())), precision=None):
    return lax.dot_general(a, b, dims, precision=precision, preferred_element_type=F32)


def flip(index, mask, bits):
    total = 0
    for bit in range(bits):
        total = total + ((index // 2**bit + mask // 2**bit) % 2) * 2**bit
    return total


def route_kernel(per_expert, hidden_ref, wr_ref, ids_ref, pos_ref, gate_ref, prob_ref, stat_ref):
    n_experts = wr_ref.shape[0]
    rows = hidden_ref.shape[0]
    block = min(512, rows)
    iota_e = lax.broadcasted_iota(jnp.int32, (n_experts, block), 0)
    upper = (lax.broadcasted_iota(jnp.int32, (block, block), 0) < lax.broadcasted_iota(jnp.int32, (block, block), 1)).astype(BF16)
    ones = jnp.ones((8, block), BF16)
    ones_f = jnp.ones((8, block), F32)
    wr = wr_ref[...]
    wr_hi = wr.astype(BF16)
    rest = wr - wr_hi.astype(F32)
    wr_mid = rest.astype(BF16)
    wr_lo = (rest - wr_mid.astype(F32)).astype(BF16)
    carry = jnp.zeros((n_experts, 1), F32)
    counts = jnp.zeros((8, n_experts), F32)
    probs = jnp.zeros((8, n_experts), F32)
    for i in range(rows // block):
        cols = pl.ds(i * block, block)
        h = hidden_ref[cols, :]
        z = dot(wr_lo, h, NT) + dot(wr_mid, h, NT) + dot(wr_hi, h, NT)
        e = jnp.exp(z - jnp.max(z, axis=0, keepdims=True))
        p = e / jnp.sum(e, axis=0, keepdims=True)
        prob_ref[:, cols] = p
        id0 = ids_ref[0:1, cols]
        id1 = ids_ref[1:2, cols]
        hit0 = iota_e == id0
        hit1 = iota_e == id1
        p0 = jnp.sum(jnp.where(hit0, p, 0.0), axis=0, keepdims=True)
        p1 = jnp.sum(jnp.where(hit1, p, 0.0), axis=0, keepdims=True)
        den = p0 + p1
        gate_ref[0:1, cols] = p0 / den
        gate_ref[1:2, cols] = p1 / den
        hits = jnp.where(hit0 | hit1, 1.0, 0.0).astype(F32)
        hits_b = hits.astype(BF16)
        rank = dot(hits_b, upper) + carry
        r0 = jnp.sum(jnp.where(hit0, rank, 0.0), axis=0, keepdims=True)
        r1 = jnp.sum(jnp.where(hit1, rank, 0.0), axis=0, keepdims=True)
        pos_ref[0:1, cols] = id0 * per_expert + r0.astype(jnp.int32)
        pos_ref[1:2, cols] = id1 * per_expert + r1.astype(jnp.int32)
        carry = carry + jnp.sum(hits, axis=1, keepdims=True)
        counts = counts + dot(ones, hits_b, NT)
        probs = probs + dot(ones_f, p, NT, HI)
    stat_ref[:, 0:n_experts] = counts
    stat_ref[:, n_experts:2 * n_experts] = probs


def scatter_kernel(steps, pos_ref, gate_ref, hidden_ref, dout_ref, send_ref, xf_ref, mf_ref, slots_ref):
    step = pl.program_id(0)
    block, d = hidden_ref.shape
    tile = send_ref.shape[0]

    @pl.when(step < steps)
    def _():
        xf_ref[...] = hidden_ref[...].astype(F32)
        mf_ref[...] = OUT_SCALE * dout_ref[...].astype(F32)

        def one(i, _):
            n = step * block + i
            x = xf_ref[pl.ds(i, 1), :]
            m = mf_ref[pl.ds(i, 1), :]
            for k in range(2):
                q = pos_ref[k, n]
                slots_ref[pl.ds(q, 1), 0:d] = x
                slots_ref[pl.ds(q, 1), d:2 * d] = gate_ref[k, n] * m
            return 0

        lax.fori_loop(0, block, one, 0, unroll=8)

    @pl.when(step >= steps)
    def _():
        start = pl.multiple_of((step - steps) * tile, tile)
        send_ref[...] = slots_ref[pl.ds(start, tile), :].astype(BF16)


def expert_kernel(
    ep, etp, capacity, pair,
    send_ref, stat_ref, w1_ref, w3_ref, w2_ref,
    back_ref, g1_ref, g3_ref, g2_ref, tab_out_ref,
    x_ref, w13_ref, w2f_ref, ga13_ref, ga2_ref, ga2t_ref, xm_ref, u_ref, dab_ref, tab_ref,
    stat_send, stat_recv, w_send, w13_recv, w2_recv, x_send, x_recv, back_send, back_recv, g_send, g_recv,
):
    n_dev = ep * etp
    n_slots = x_ref.shape[0]
    rows = x_ref.shape[2]
    d = w1_ref.shape[1]
    part = w1_ref.shape[2]
    ff = w2f_ref.shape[1]
    bits = n_dev.bit_length() - 1
    etp_bits = etp.bit_length() - 1
    me_o = lax.axis_index("ep")
    me_t = lax.axis_index("etp")
    me = me_o * etp + me_t

    def where_is(peer):
        return {"ep": peer // etp, "etp": peer % etp}

    def remote(src, dst, send, recv, peer):
        pltpu.make_async_remote_copy(src_ref=src, dst_ref=dst, send_sem=send, recv_sem=recv, device_id=where_is(peer), device_id_type=MESH).start()

    def wait_bytes(ref, sem):
        pltpu.make_async_copy(ref, ref, sem).wait()

    barrier = pltpu.get_barrier_semaphore()

    def hello(i, _):
        pl.semaphore_signal(barrier, inc=1, device_id=where_is((me + i) % n_dev), device_id_type=MESH)
        return 0

    lax.fori_loop(1, n_dev, hello, 0)
    pl.semaphore_wait(barrier, n_dev - 1)

    def order(i):
        return flip(me, (i * 11) % n_dev, bits)

    def send_stats(i, _):
        remote(stat_ref, tab_ref.at[me], stat_send, stat_recv, order(i))
        return 0

    lax.fori_loop(1, n_dev, send_stats, 0)
    tab_ref[me] = stat_ref[...]

    def lanes(offset, t):
        return pl.ds(pl.multiple_of(offset + t * part, part), part)

    def send_slot(j, _):
        mine = me_t * n_slots + j
        pltpu.make_async_copy(w1_ref.at[mine], w13_ref.at[j, :, lanes(0, me_t)], w13_recv.at[j]).start()
        pltpu.make_async_copy(w3_ref.at[mine], w13_ref.at[j, :, lanes(ff, me_t)], w13_recv.at[j]).start()
        pltpu.make_async_copy(w2_ref.at[mine], w2f_ref.at[j, lanes(0, me_t), :], w2_recv.at[j]).start()

        def weights(i, _):
            t = flip(me_t, i, etp_bits)
            peer = me_o * etp + t
            theirs = t * n_slots + j
            remote(w1_ref.at[theirs], w13_ref.at[j, :, lanes(0, me_t)], w_send, w13_recv.at[j], peer)
            remote(w3_ref.at[theirs], w13_ref.at[j, :, lanes(ff, me_t)], w_send, w13_recv.at[j], peer)
            remote(w2_ref.at[theirs], w2f_ref.at[j, lanes(0, me_t), :], w_send, w2_recv.at[j], peer)
            return 0

        lax.fori_loop(1, etp, weights, 0)
        pltpu.make_async_copy(send_ref.at[me * n_slots + j], x_ref.at[j, me], x_recv.at[j]).start()

        def tokens(i, _):
            peer = order(i)
            remote(send_ref.at[peer * n_slots + j], x_ref.at[j, me], x_send, x_recv.at[j], peer)
            return 0

        lax.fori_loop(1, n_dev, tokens, 0)
        return 0

    lax.fori_loop(0, n_slots, send_slot, 0)

    wait_bytes(tab_ref.at[0:n_dev - 1], stat_recv)
    tab_out_ref[...] = tab_ref[...]
    table = tab_ref[:, 0, :]
    shape = table.shape
    below = (lax.broadcasted_iota(jnp.int32, (n_dev, n_dev), 1) < lax.broadcasted_iota(jnp.int32, (n_dev, n_dev), 0)).astype(F32)
    keep = jnp.minimum(table, capacity - dot(below, table, precision=HI))
    src_iota = lax.broadcasted_iota(jnp.int32, shape, 0)
    lane_iota = lax.broadcasted_iota(jnp.int32, shape, 1)
    row_iota = lax.broadcasted_iota(jnp.int32, (rows, 2 * d), 0).astype(F32)
    n_blocks = n_dev // pair
    block_bits = n_blocks.bit_length() - 1

    def give_back(j, src):
        @pl.when(src == me)
        def _():
            pltpu.make_async_copy(x_ref.at[j, me], back_ref.at[me * n_slots + j], back_recv).start()

        @pl.when(src != me)
        def _():
            remote(x_ref.at[j, src], back_ref.at[me * n_slots + j], back_send, back_recv, src)

    def do_slot(j, _):
        wait_bytes(w13_ref.at[j], w13_recv.at[j])
        wait_bytes(w2f_ref.at[j], w2_recv.at[j])
        wait_bytes(x_ref.at[j], x_recv.at[j])
        ga13_ref[j] = jnp.zeros((d, 2 * ff), F32)
        ga2t_ref[...] = jnp.zeros((d, ff), F32)

        def first_of(b):
            return flip(me // pair, b, block_bits) * pair

        def do_block(b, _):
            first = first_of(b)
            for s in range(pair):
                limit = jnp.sum(jnp.where((src_iota == first + s) & (lane_iota == me * n_slots + j), keep, 0.0), keepdims=True)
                full = x_ref[j, first + s].astype(F32)
                xm_ref[s * rows:(s + 1) * rows, :] = jnp.where(row_iota < limit, full, 0.0).astype(BF16)
            x = xm_ref[:, 0:d]
            c = xm_ref[:, d:2 * d]
            for q in range(ff // part):
                here = slice(q * part, (q + 1) * part)
                there = slice(ff + q * part, ff + (q + 1) * part)
                a = dot(x, w13_ref[j, :, here])
                v = dot(x, w13_ref[j, :, there])
                du = dot(c, w2f_ref[j, here, :], NT)
                sig = jax.nn.sigmoid(a)
                silu = a * sig
                u_ref[:, here] = (silu * v).astype(BF16)
                dab_ref[:, here] = (du * v * sig * (1.0 + a * (1.0 - sig))).astype(BF16)
                dab_ref[:, there] = (du * silu).astype(BF16)
            y = dot(u_ref[...], w2f_ref[j]).astype(BF16)
            dx = dot(dab_ref[...], w13_ref[j], NT).astype(BF16)
            for s in range(pair):
                x_ref[j, first + s, :, 0:d] = y[s * rows:(s + 1) * rows]
                x_ref[j, first + s, :, d:2 * d] = dx[s * rows:(s + 1) * rows]
            ga13_ref[j] += dot(x, dab_ref[...], TN)
            ga2t_ref[...] += dot(c, u_ref[...], TN)

            @pl.when(b > 0)
            def _():
                for s in range(pair):
                    give_back(j, first_of(b - 1) + s)

            return 0

        lax.fori_loop(0, n_blocks, do_block, 0)
        ga2_ref[j] = ga2t_ref[...].T
        for s in range(pair):
            give_back(j, first_of(n_blocks - 1) + s)

        mine = me_t * n_slots + j
        pltpu.make_async_copy(ga13_ref.at[j, :, lanes(0, me_t)], g1_ref.at[mine], g_recv.at[0]).start()
        pltpu.make_async_copy(ga13_ref.at[j, :, lanes(ff, me_t)], g3_ref.at[mine], g_recv.at[1]).start()
        pltpu.make_async_copy(ga2_ref.at[j, lanes(0, me_t), :], g2_ref.at[mine], g_recv.at[2]).start()

        def grads(i, _):
            t = flip(me_t, i, etp_bits)
            peer = me_o * etp + t
            remote(ga13_ref.at[j, :, lanes(0, t)], g1_ref.at[mine], g_send, g_recv.at[0], peer)
            remote(ga13_ref.at[j, :, lanes(ff, t)], g3_ref.at[mine], g_send, g_recv.at[1], peer)
            remote(ga2_ref.at[j, lanes(0, t), :], g2_ref.at[mine], g_send, g_recv.at[2], peer)
            return 0

        lax.fori_loop(1, etp, grads, 0)
        return 0

    lax.fori_loop(0, n_slots, do_slot, 0)

    others = (n_dev - 1) * n_slots
    wait_bytes(tab_ref.at[0:n_dev - 1], stat_send)
    for _ in range(3):
        wait_bytes(w1_ref.at[0:(etp - 1) * n_slots], w_send)
    wait_bytes(send_ref.at[0:others], x_send)
    wait_bytes(send_ref.at[0:others], back_send)
    for _ in range(3):
        wait_bytes(g1_ref.at[0:(etp - 1) * n_slots], g_send)
    wait_bytes(back_ref, back_recv)
    wait_bytes(g1_ref, g_recv.at[0])
    wait_bytes(g3_ref, g_recv.at[1])
    wait_bytes(g2_ref, g_recv.at[2])


def combine_kernel(
    n_tokens, chunk,
    pos_ref, gates_ref, back_ref, tab_ref, wr_ref, hidden_ref, dout_ref, ids_ref, gate_ref, prob_ref,
    out_ref, dh_ref, dwr_ref, aux_ref,
    rows_ref, stage_ref, y_ref, mix_ref, sem,
):
    step = pl.program_id(0)
    block, d = hidden_ref.shape
    n_experts = wr_ref.shape[0]
    n_chunks = rows_ref.shape[0] // chunk

    totals = jnp.sum(tab_ref[:, 0:1, :], axis=0)
    frac = totals[:, 0:n_experts] / (2 * n_tokens)

    def fetch(i, slot):
        start = pl.multiple_of(i * chunk, chunk)
        return pltpu.make_async_copy(back_ref.at[pl.ds(start, chunk), :], stage_ref.at[slot], sem.at[slot])

    @pl.when(step == 0)
    def _():
        fetch(0, 0).start()

        def body(i, _):
            slot = i % 2

            @pl.when(i + 1 < n_chunks)
            def _():
                fetch(i + 1, 1 - slot).start()

            fetch(i, slot).wait()
            rows_ref[pl.ds(pl.multiple_of(i * chunk, chunk), chunk), :] = stage_ref[slot].astype(F32)
            return 0

        lax.fori_loop(0, n_chunks, body, 0)
        dwr_ref[...] = jnp.zeros_like(dwr_ref)
        mean_prob = totals[:, n_experts:2 * n_experts] / n_tokens
        aux_ref[0, 0] = AUX_COEF * n_experts * jnp.sum(frac * mean_prob)

    def one(i, _):
        n = step * block + i
        r0 = rows_ref[pl.ds(pos_ref[0, n], 1), :]
        r1 = rows_ref[pl.ds(pos_ref[1, n], 1), :]
        y0, y1 = r0[:, 0:d], r1[:, 0:d]
        y_ref[pl.ds(i, 1), 0:d] = y0
        y_ref[pl.ds(i, 1), d:2 * d] = y1
        mix_ref[pl.ds(i, 1), 0:d] = gates_ref[0, n] * y0 + gates_ref[1, n] * y1
        mix_ref[pl.ds(i, 1), d:2 * d] = r0[:, d:2 * d] + r1[:, d:2 * d]
        return 0

    lax.fori_loop(0, block, one, 0, unroll=8)

    h = hidden_ref[...].astype(F32)
    dy = dout_ref[...].astype(F32)
    m = OUT_SCALE * dy
    out_ref[...] = (h + OUT_SCALE * mix_ref[:, 0:d]).astype(BF16)

    ones = jnp.ones((8, d), F32)
    dg0 = dot(ones, m * y_ref[:, 0:d], NT, HI)[0:1]
    dg1 = dot(ones, m * y_ref[:, d:2 * d], NT, HI)[0:1]
    p = prob_ref[...]
    iota_e = lax.broadcasted_iota(jnp.int32, p.shape, 0)
    hit0 = iota_e == ids_ref[0:1, :]
    hit1 = iota_e == ids_ref[1:2, :]
    den = jnp.sum(jnp.where(hit0 | hit1, p, 0.0), axis=0, keepdims=True)
    mean = gate_ref[0:1, :] * dg0 + gate_ref[1:2, :] * dg1
    eye = lax.broadcasted_iota(jnp.int32, (n_experts, n_experts), 0) == lax.broadcasted_iota(jnp.int32, (n_experts, n_experts), 1)
    ct = (AUX_COEF * n_experts / n_tokens) * jnp.sum(jnp.where(eye, frac, 0.0), axis=1, keepdims=True)
    dp = jnp.where(hit0, (dg0 - mean) / den, 0.0) + jnp.where(hit1, (dg1 - mean) / den, 0.0) + ct
    dz = p * (dp - jnp.sum(p * dp, axis=0, keepdims=True))
    dwr_ref[...] += dot(dz, h, precision=HI)
    dh_ref[...] = (dy + mix_ref[:, d:2 * d] + dot(dz, wr_ref[...], TN, HI)).astype(BF16)


def sum_kernel(ep, etp, part_ref, out_ref, box_ref, mine_ref, all_ref, send1, recv1, send2, recv2):
    n_dev = ep * etp
    across = part_ref.shape[1] // 128
    me = lax.axis_index("ep") * etp + lax.axis_index("etp")

    def where_is(peer):
        return {"ep": peer // etp, "etp": peer % etp}

    def tile(ref, i):
        return ref.at[pl.ds(pl.multiple_of((i // across) * 8, 8), 8), pl.ds(pl.multiple_of((i % across) * 128, 128), 128)]

    def wait_bytes(ref, sem):
        pltpu.make_async_copy(ref, ref, sem).wait()

    barrier = pltpu.get_barrier_semaphore()

    def hello(i, _):
        pl.semaphore_signal(barrier, inc=1, device_id=where_is((me + i) % n_dev), device_id_type=MESH)
        return 0

    lax.fori_loop(1, n_dev, hello, 0)
    pl.semaphore_wait(barrier, n_dev - 1)

    def first(i, _):
        peer = (me + i) % n_dev
        pltpu.make_async_remote_copy(tile(part_ref, peer), box_ref.at[me], send1, recv1, device_id=where_is(peer), device_id_type=MESH).start()
        return 0

    lax.fori_loop(1, n_dev, first, 0)
    pltpu.make_async_copy(tile(part_ref, me), box_ref.at[me], recv1).start()
    wait_bytes(box_ref, recv1)
    mine_ref[...] = jnp.sum(box_ref[...], axis=0)

    def second(i, _):
        peer = (me + i) % n_dev
        pltpu.make_async_remote_copy(mine_ref, all_ref.at[me], send2, recv2, device_id=where_is(peer), device_id_type=MESH).start()
        return 0

    lax.fori_loop(1, n_dev, second, 0)
    all_ref[me] = mine_ref[...]
    wait_bytes(all_ref.at[0:n_dev - 1], recv2)
    for i in range(n_dev):
        out_ref[(i // across) * 8:(i // across) * 8 + 8, (i % across) * 128:(i % across) * 128 + 128] = all_ref[i]
    wait_bytes(box_ref.at[0:n_dev - 1], send1)
    wait_bytes(all_ref.at[0:n_dev - 1], send2)


def solution(mesh):
    ep_size = mesh.shape["ep"]
    etp_size = mesh.shape["etp"]
    n_dev = ep_size * etp_size
    all_axes = ("ep", "etp")
    tok_spec = P(all_axes, None)
    gate_spec = P("ep", None, "etp")
    down_spec = P("ep", "etp", None)

    def layer(hidden, w_router, expert_ids, d_out, w_gate, w_up, w_down):
        rows, d = hidden.shape
        n_experts = w_router.shape[1]
        n_tokens = rows * n_dev
        capacity = (5 * n_tokens + 2 * n_experts - 1) // (2 * n_experts)
        per_expert = 7 * rows // (2 * n_experts)
        n_slots = n_experts // n_dev
        local_experts, _, part = w_gate.shape
        ff = part * etp_size
        all_slots = n_experts * per_expert
        ids_t = expert_ids.T
        wr_t = w_router.T

        vmem = pl.BlockSpec(memory_space=pltpu.VMEM)
        smem = pl.BlockSpec(memory_space=pltpu.SMEM)
        anywhere = pl.BlockSpec(memory_space=pl.ANY)
        big = 60 * 1024 * 1024

        pos, gates, probs, stats = pl.pallas_call(
            functools.partial(route_kernel, per_expert),
            out_shape=(
                jax.ShapeDtypeStruct((2, rows), jnp.int32),
                jax.ShapeDtypeStruct((2, rows), F32),
                jax.ShapeDtypeStruct((n_experts, rows), F32),
                jax.ShapeDtypeStruct((8, 2 * n_experts), F32),
            ),
            in_specs=[vmem] * 3,
            out_specs=(vmem,) * 4,
            name="route",
        )(hidden, wr_t, ids_t)

        block = min(512, rows)
        steps = rows // block
        tile = n_slots * per_expert
        tiles = all_slots // tile
        send = pl.pallas_call(
            functools.partial(scatter_kernel, steps),
            out_shape=jax.ShapeDtypeStruct((all_slots, 2 * d), BF16),
            grid=(steps + tiles,),
            in_specs=[
                smem, smem,
                pl.BlockSpec((block, d), lambda i: (jnp.minimum(i, steps - 1), 0)),
                pl.BlockSpec((block, d), lambda i: (jnp.minimum(i, steps - 1), 0)),
            ],
            out_specs=pl.BlockSpec((tile, 2 * d), lambda i: (jnp.maximum(i - steps, 0), 0)),
            scratch_shapes=[pltpu.VMEM((block, d), F32), pltpu.VMEM((block, d), F32), pltpu.VMEM((all_slots, 2 * d), F32)],
            compiler_params=pltpu.CompilerParams(vmem_limit_bytes=big),
            name="scatter",
        )(pos, gates, hidden, d_out)
        send = send.reshape(n_experts, per_expert, 2 * d)

        pair = 2
        dma = pltpu.SemaphoreType.DMA
        grad = jax.ShapeDtypeStruct((local_experts, d, part), F32)
        back, g_gate, g_up, g_down, table = pl.pallas_call(
            functools.partial(expert_kernel, ep_size, etp_size, float(capacity), pair),
            out_shape=(
                jax.ShapeDtypeStruct((n_experts, per_expert, 2 * d), BF16),
                grad, grad,
                jax.ShapeDtypeStruct((local_experts, part, d), F32),
                jax.ShapeDtypeStruct((n_dev, 8, 2 * n_experts), F32),
            ),
            in_specs=[anywhere, vmem, anywhere, anywhere, anywhere],
            out_specs=(anywhere,) * 4 + (vmem,),
            scratch_shapes=[
                pltpu.VMEM((n_slots, n_dev, per_expert, 2 * d), BF16),
                pltpu.VMEM((n_slots, d, 2 * ff), BF16),
                pltpu.VMEM((n_slots, ff, d), BF16),
                pltpu.VMEM((n_slots, d, 2 * ff), F32),
                pltpu.VMEM((n_slots, ff, d), F32),
                pltpu.VMEM((d, ff), F32),
                pltpu.VMEM((pair * per_expert, 2 * d), BF16),
                pltpu.VMEM((pair * per_expert, ff), BF16),
                pltpu.VMEM((pair * per_expert, 2 * ff), BF16),
                pltpu.VMEM((n_dev, 8, 2 * n_experts), F32),
                dma, dma, dma, dma((n_slots,)), dma((n_slots,)), dma, dma((n_slots,)), dma, dma, dma, dma((3,)),
            ],
            compiler_params=pltpu.CompilerParams(collective_id=0, has_side_effects=True, vmem_limit_bytes=big),
            name="experts",
        )(send, stats, w_gate, w_up, w_down)

        cols = lambda n: pl.BlockSpec((n, block), lambda i: (0, i))
        tok = pl.BlockSpec((block, d), lambda i: (i, 0))
        output, d_hidden, dwr_part, aux_loss = pl.pallas_call(
            functools.partial(combine_kernel, n_tokens, tile),
            out_shape=(
                jax.ShapeDtypeStruct((rows, d), BF16),
                jax.ShapeDtypeStruct((rows, d), BF16),
                jax.ShapeDtypeStruct((n_experts, d), F32),
                jax.ShapeDtypeStruct((1, 1), F32),
            ),
            grid=(steps,),
            in_specs=[smem, smem, anywhere, vmem, vmem, tok, tok, cols(2), cols(2), cols(n_experts)],
            out_specs=(tok, tok, pl.BlockSpec((n_experts, d), lambda i: (0, 0)), smem),
            scratch_shapes=[
                pltpu.VMEM((all_slots, 2 * d), F32),
                pltpu.VMEM((2, tile, 2 * d), BF16),
                pltpu.VMEM((block, 2 * d), F32),
                pltpu.VMEM((block, 2 * d), F32),
                dma((2,)),
            ],
            compiler_params=pltpu.CompilerParams(vmem_limit_bytes=big),
            name="combine",
        )(pos, gates, back.reshape(all_slots, 2 * d), table, wr_t, hidden, d_out, ids_t, gates, probs)

        dwr = pl.pallas_call(
            functools.partial(sum_kernel, ep_size, etp_size),
            out_shape=jax.ShapeDtypeStruct((n_experts, d), F32),
            in_specs=[vmem],
            out_specs=vmem,
            scratch_shapes=[
                pltpu.VMEM((n_dev, 8, 128), F32), pltpu.VMEM((8, 128), F32), pltpu.VMEM((n_dev, 8, 128), F32),
                dma, dma, dma, dma,
            ],
            compiler_params=pltpu.CompilerParams(collective_id=1, has_side_effects=True),
            name="sum_router",
        )(dwr_part)
        return output, d_hidden, dwr.T, aux_loss.reshape(()), g_gate, g_up, g_down

    return jax.shard_map(layer, mesh=mesh, in_specs=(tok_spec, P(), tok_spec, tok_spec, gate_spec, gate_spec, down_spec), out_specs=(tok_spec, tok_spec, P(), P(), gate_spec, gate_spec, down_spec), check_vma=False)
```

time: 2270 us -> 700 us (0.31)
  waiting for transfers between devices: 1010 us -> 0 us
  Pallas kernels: 0 us -> 687 us
  local copies, waits for them, and re-layouts: 413 us -> 11.9 us
  matrix products: 321 us -> 0 us
  other arithmetic: 246 us -> 0 us
  blocking collectives: 237 us -> 0 us
    reduce_scatter x2 -> x0, waiting for transfers between devices: 813 us -> none  [combine(): lax.psum_scatter(part_out, 'etp', scatter_dimension=1, tiled=True)]
    pallas_call x0 -> x5, Pallas kernels: none -> 687 us  [the longest x1 548 us: layer(): pl.pallas_call(functools.partial(expert_kernel, ep_size, etp_size, float(...]
    dot_general x12 -> x0, matrix products: 321 us -> none  [the longest x1 76 us: layer(): jnp.einsum('erd,efd->erf', dy_in, w_down, preferred_element_type=jnp.floa...]
    gather x15 -> x0, local copies, waits for them, and re-layouts: 260 us -> none  [the longest x2 111 us: dispatch(): jnp.take(values, row_index, axis=0, mode='fill', fill_value=0)]
    all_gather x2 -> x0, waiting for transfers between devices: 200 us -> none  [dispatch(): return lax.all_gather(received, 'etp', axis=1, tiled=True)]
    all_to_all x2 -> x0, blocking collectives: 170 us -> none  [dispatch(): received = lax.all_to_all(send_buf, 'ep', 0, 1, tiled=True)]
    reduce_sum x11 -> x0, other arithmetic: 60.2 us -> none  [the longest x1 25 us: layer(): jnp.sum(dx_pair, axis=1, dtype=jnp.float32)]
    unnamed x4 -> x0, other arithmetic: 45 us -> none
  transfers between devices with their start and end apart: 7 -> 0, of which waited for: 3 -> 0; matrix products, arithmetic and copies ran while one was open for 29% -> 0% of each run, Pallas kernels for 0% -> 0%
where the time goes in v1:
time: 700 us
  Pallas kernels  687 us (98%)
  local copies, waits for them, and re-layouts  11.9 us (2%)
    pallas_call x1, Pallas kernels, layer(): pl.pallas_call(functools.partial(expert_kernel, ep_size, etp_size, float(...  548 us
    pallas_call x1, Pallas kernels, layer(): pl.pallas_call(functools.partial(combine_kernel, n_tokens, tile), out_sha...  66.4 us
    pallas_call x1, Pallas kernels, layer(): pl.pallas_call(functools.partial(scatter_kernel, steps), out_shape=jax.Sh...  53.9 us

profile of v1, /device:TPU:0, one launch (start us, length us, event | category | flops | bytes accessed | tf_op | source)
XLA Modules:
  0.0 699.5 jit_solution(7024149554364309884)
XLA Ops:
  0.6 6.4 route.1
  7.1 53.9 %scatter.1 = bf16[14336,512]{1,0:T(8,128)(2,1)} custom-call(s32[2,4096]{1,0:T(2,128)} %get-tuple-element.20.pos_ref, f32[2,4096]{1,0:T(2,128)} %get-tuple-element.21.gate_ref.gates_ref, bf16[4096,256]{1,0:T(8,128)(2,1)} %hidden_ref.5, bf16[4096,256]{1,0:T(8,128)(2,1)} %dout_ref.3), custom_call_target="tpu_custom_call" | custom-call | tf_op jit(solution)/shard_map/scatter/pallas_call | solution.py:448
  60.9 547.9 %experts.1 = (bf16[64,224,512]{2,1,0:T(8,128)(2,1)}, f32[16,256,256]{2,1,0:T(8,128)}, f32[16,256,256]{2,1,0:T(8,128)}, f32[16,256,256]{2,1,0:T(8,128)}, f32[16,8,128]{2,1,0:T(8,128)}) custom-call(bf16[64,224,512]{2,1,0:T(8,128)(2,1)} %bitcast.6, f32[8,128]{1,0:T(8,128)} %get-tuple-element.22.stat_ref, bf16[16,256,256]{2,1,0:T(8,128)(2,1)} %w1_ref.1, ...), custom_call_target="tpu_custom_call" | custom-call | tf_op jit(solution)/shard_map/experts/pallas_call | solution.py:467
  608.8 66.4 %combine.1 = (bf16[4096,256]{1,0:T(8,128)(2,1)}, bf16[4096,256]{1,0:T(8,128)(2,1)}, f32[64,256]{1,0:T(8,128)}, f32[1,1]{1,0:T(1,128)}) custom-call(s32[2,4096]{1,0:T(2,128)} %get-tuple-element.20.pos_ref, f32[2,4096]{1,0:T(2,128)} %get-tuple-element.21.gate_ref.gates_ref, bf16[14336,512]{1,0:T(8,128)(2,1)} %bitcast.7, ...), custom_call_target="tpu_custom_call" | custom-call | tf_op jit(solution)/shard_map/combine/pallas_call | solution.py:496
  675.2 12.4 %sum_router.1 = f32[64,256]{1,0:T(8,128)} custom-call(f32[64,256]{1,0:T(8,128)} %get-tuple-element.28.part_ref), custom_call_target="tpu_custom_call" | custom-call | tf_op jit(solution)/shard_map/sum_router/pallas_call | solution.py:518
  687.6 1.5 copy.18
  689.1 0.0 copy-start.1
  689.1 4.7 copy.19
  693.8 0.0 copy-done.1
  693.8 0.0 copy-start
  693.8 2.1 copy.20
  695.9 1.6 copy-done
  697.5 2.0 copy.21
Async XLA Ops:
  689.1 4.8 copy-start.1
  693.8 3.7 copy-start
